TPU v7x, 32 devices: a whole 2x2x4 slice. The times are simulated.
32 devices in a mesh: seq: 8 (over z, y), grp: 4 (over x, core).
Axes of the slice: x: 2, y: 2, z: 4, core: 2. Of those that a mesh axis runs over, the one named last changes fastest.
Arguments:
- tokens: bfloat16 [4096, 2560], P('seq'), may hold values from -6 to 6
- norm_gain: float32 [2560], replicated, may hold values from 0.25 to 1.75
- inner_weight: bfloat16 [2560, 2, 5120], P(None, None, ('grp', 'seq')), may hold values from -0.125 to 0.125
- state_weight: bfloat16 [2560, 2, 128], replicated, may hold values from -0.125 to 0.125
- step_weight: bfloat16 [2560, 80], P(None, 'grp'), may hold values from -0.125 to 0.125
- step_bias: float32 [80], P('grp'), may hold values from -1 to 1
- decay_rate: float32 [80], P('grp'), may hold values from 4.8828124e-06 to 0.05
- skip_scale: float32 [80], P('grp'), may hold values from 0.5 to 1.5
- conv_inner: bfloat16 [4, 5120], P(None, 'grp'), may hold values from -3 to 3
- conv_state: bfloat16 [4, 2, 128], replicated, may hold values from -3 to 3
- out_gain: float32 [5120], P('grp'), may hold values from 0.25 to 1.75
- out_weight: bfloat16 [5120, 2560], P(None, 'grp'), may hold values from -0.078125 to 0.078125
Outputs:
- mixed: bfloat16 [4096, 2560], P('seq', 'grp')
All inputs are finite; a program needn't handle non-finite values.
Results may differ from a plain program's by a relative error of at most 0.0075.
Values may be sent and summed in bfloat16 or wider, within the bound.
No kernel may reach another device: no remote copies, remote signals or barrier semaphores. Data moves between devices by JAX's collectives and lax.ppermute only.
A program may use at most 64 MiB of HBM per device.

v0:
```python
from functools import partial
import jax
import jax.numpy as jnp
from jax import lax
from jax.sharding import PartitionSpec as P

SPAN = 256
EPS = 1e-05
HIGH = lax.Precision.HIGHEST


def from_behind(value, axis, steps):
    count = lax.axis_size(axis)
    leading, last = (max(0, -steps), min(count, count - steps))
    return lax.ppermute(value, axis, [(source, source + steps) for source in range(leading, last)])


def prefix(value, axis, combine, identity):
    length, place = (lax.axis_size(axis), lax.axis_index(axis))
    everything = jax.tree.map(lambda part: lax.all_gather(part, axis), value)
    start = jax.tree.map(
        lambda part, zero: jnp.broadcast_to(jnp.asarray(zero, part.dtype), part.shape),
        value,
        identity,
    )

    def step(k, before):
        reached = k < place
        new = combine(before, jax.tree.map(lambda part: part[k], everything))
        return jax.tree.map(lambda a, b: jnp.where(reached, a, b), new, before)

    return lax.fori_loop(0, length, step, start)


def conv_rows(before, current, weight):
    width = weight.shape[0]
    padded = jnp.concatenate([before, current], axis=0).astype(jnp.float32)
    length = current.shape[0]
    total = jnp.zeros(current.shape, jnp.float32)
    for offset in range(width):
        total = total + weight[offset].astype(jnp.float32) * padded[offset : offset + length]
    return jax.nn.silu(total).astype(jnp.bfloat16)


def span_step(rate, skip, state, inputs):
    xvals, bmat, cmat, delta = inputs
    logdec = -delta * rate[None, :]
    cumul = jnp.cumsum(logdec, axis=0)
    length = cumul.shape[0]
    scores = jnp.einsum("tn,sn->ts", cmat, bmat, preferred_element_type=jnp.float32)
    lower = jnp.arange(length)[:, None] >= jnp.arange(length)[None, :]
    diffs = cumul.T[:, :, None] - cumul.T[:, None, :]
    decay = jnp.exp(jnp.where(lower[None], diffs, -jnp.inf))
    mixer = (scores[None] * decay * delta.T[:, None, :]).astype(jnp.bfloat16)
    intra = jnp.einsum("hts,shp->thp", mixer, xvals, preferred_element_type=jnp.float32)
    inter = jnp.exp(cumul)[:, :, None] * jnp.einsum(
        "tn,hpn->thp", cmat.astype(jnp.float32), state, precision=HIGH
    )
    output = intra + inter + skip[None, :, None] * xvals.astype(jnp.float32)
    tail = jnp.exp(cumul[-1][None, :] - cumul) * delta
    weighted = (tail[:, :, None] * bmat.astype(jnp.float32)[:, None, :]).astype(jnp.bfloat16)
    update = jnp.einsum("shp,shn->hpn", xvals, weighted, preferred_element_type=jnp.float32)
    new_state = jnp.exp(cumul[-1])[:, None, None] * state + update
    return (new_state, output)


def body(
    tokens,
    norm_gain,
    inner_weight,
    state_weight,
    step_weight,
    step_bias,
    decay_rate,
    skip_scale,
    conv_inner,
    conv_state,
    out_gain,
    out_weight,
):
    tok_rows = tokens.shape[0]
    model_width = tokens.shape[1]
    wide = tokens.astype(jnp.float32)
    normed = (
        wide * lax.rsqrt(jnp.mean(wide * wide, axis=1, keepdims=True) + EPS) * norm_gain
    ).astype(jnp.bfloat16)
    piece = lax.all_gather(inner_weight, "seq", axis=2, tiled=True)
    count = piece.shape[2]
    flat = piece.reshape(piece.shape[0], 2 * count)
    result = jnp.dot(normed, flat, preferred_element_type=jnp.float32).astype(jnp.bfloat16)
    inner = result.reshape(tok_rows, 2, count)
    state_flat = state_weight.reshape(model_width, -1)
    state_pre = (
        jnp.dot(normed, state_flat, preferred_element_type=jnp.float32)
        .astype(jnp.bfloat16)
        .reshape(tok_rows, 2, -1)
    )
    delta = jax.nn.softplus(
        jnp.dot(normed, step_weight, preferred_element_type=jnp.float32) + step_bias
    )
    inner_values = inner[:, 0, :]
    width = conv_inner.shape[0]
    first_kept = tok_rows - width + 1
    before_values, before_state = from_behind(
        (inner_values[first_kept:], state_pre[first_kept:]), "seq", 1
    )
    values = conv_rows(before_values, inner_values, conv_inner)
    conv_out = conv_rows(before_state, state_pre, conv_state)
    heads_here = delta.shape[1]
    head_width = values.shape[1] // heads_here
    state_width = conv_out.shape[2]
    blocks = tok_rows // SPAN
    xs_blocks = values.reshape(blocks, SPAN, heads_here, head_width)
    b_blocks = conv_out[:, 0, :].reshape(blocks, SPAN, state_width)
    c_blocks = conv_out[:, 1, :].reshape(blocks, SPAN, state_width)
    d_blocks = delta.reshape(blocks, SPAN, heads_here)
    initial = jnp.zeros((heads_here, head_width, state_width), jnp.float32)
    final_state, outputs = lax.scan(
        partial(span_step, decay_rate, skip_scale),
        initial,
        (xs_blocks, b_blocks, c_blocks, d_blocks),
    )
    cumdev = jnp.cumsum(-delta * decay_rate[None, :], axis=0)
    totals = cumdev[-1]

    def combine(earlier, later):
        return (earlier[0] + later[0], jnp.exp(later[0])[:, None, None] * earlier[1] + later[1])

    scanned = prefix(
        (totals, final_state), "seq", combine, (jnp.zeros_like(totals), jnp.zeros_like(final_state))
    )
    incoming = scanned[1]
    cmat_wide = conv_out[:, 1, :].astype(jnp.float32)
    carried = jnp.exp(cumdev)[:, :, None] * jnp.einsum(
        "tn,hpn->thp", cmat_wide, incoming, precision=HIGH
    )
    mixed_heads = (outputs.reshape(tok_rows, heads_here, head_width) + carried).reshape(
        tok_rows, heads_here * head_width
    )
    gated = mixed_heads * jax.nn.silu(inner[:, 1, :].astype(jnp.float32))
    squares = lax.psum(jnp.sum(gated * gated, axis=1), "grp")
    row_scale = lax.rsqrt(squares / (lax.axis_size("grp") * gated.shape[1]) + EPS)
    scaled = (gated * out_gain).astype(jnp.bfloat16)
    summed = jnp.dot(
        lax.all_gather(scaled, "grp", axis=1, tiled=True),
        out_weight,
        preferred_element_type=jnp.float32,
    )
    return (summed * row_scale[:, None]).astype(jnp.bfloat16)


def solution(mesh):
    return jax.shard_map(
        body,
        mesh=mesh,
        in_specs=(
            P("seq", None),
            P(),
            P(None, None, ("grp", "seq")),
            P(),
            P(None, "grp"),
            P("grp"),
            P("grp"),
            P("grp"),
            P(None, "grp"),
            P(),
            P("grp"),
            P(None, "grp"),
        ),
        out_specs=P("seq", "grp"),
        check_vma=False,
    )
```

profile of v0, /device:TPU:0, one launch (start us, length us, event | category | flops | bytes accessed | tf_op | source)
XLA Modules:
  0.0 453.3 jit_solution(12982020083999643823)
XLA Ops:
  7.3 2.4 fusion.40
  10.8 4.9 %collective-permute-start.1 = (bf16[3,2,128]{2,0,1:T(4,128)(2,1)S(1)}, bf16[3,2,128]{2,0,1:T(4,128)(2,1)S(1)}, u32[]{:S(2)}, u32[]{:S(2)}) collective-permute-start(bf16[3,2,128]{2,0,1:T(4,128)(2,1)S(1)} %slice_bitcast_fusion.2), channel_id=1, source_target_pairs={{0,4},{4,8},{8,12},{12,16},{16,20},{20,24},{24,28},{1,5},{5,9},{9,... | collective-permute-start | bytes 4616 | tf_op jit(solution)/shard_map/ppermute | solution.py:15
  16.4 1.5 compare_select_fusion.1
  20.8 174.0 %all-gather.6.cloned.1.call-done = bf16[2560,2,1280]{0,2,1:T(8,128)(2,1)} async-done(((bf16[2560,2,160]{0,2,1:T(8,128)(2,1)}), bf16[2560,2,1280]{0,2,1:T(8,128)(2,1)}) %all-gather.6.cloned.1.call-update) | async-done | bytes 13107216 | tf_op jit(solution)/shard_map/all_gather | solution.py:87
  194.8 11.2 %convolution_convert_fusion = bf16[512,2560]{1,0:T(8,128)(2,1)} fusion(bf16[2560,2560]{0,1:T(8,128)(2,1)} %bitcast.199, bf16[512,2560]{1,0:T(8,128)(2,1)S(1)} %copy-done.6, f32[2560]{0:T(1024)S(1)} %copy-done.16, f32[512]{0:T(512)S(1)} %add_rsqrt_fusion.1), kind=kOutput, calls=%fused_computation.59 | convolution fusion | flops 6717440000 | bytes 18362368 | tf_op jit(solution)/shard_map/dot_general | solution.py:90
  206.0 3.0 copy.65
  209.1 2.6 collective-permute-start
  211.8 2.0 slice_convert_fusion
  213.8 4.0 collective-permute-done
  218.5 3.2 multiply_convert_fusion.8
  222.4 71.2 %while.27 = (s32[]{:T(128)}, f32[20,64,128]{2,1,0:T(8,128)S(1)}, f32[2,256,20,64]{1,0,3,2:T(2,128)}, f32[2,256,20]{1,0,2:T(2,128)S(1)}, f32[20]{0:T(128)S(1)}, /...) while((s32[]{:T(128)}, f32[20,64,128]{2,1,0:T(8,128)S(1)}, ...), condition=%wide.region_4.5_spmd.clone, body=%wide.region_1.4_spmd.clone.sunk | while | flops 782684224 | bytes 15246184 | solution.py:118
  225.2 1.5 fusion.101
  229.1 27.0 %dynamic_update_slice.6 = f32[2,256,20,64]{1,0,3,2:T(2,128)} dynamic-update-slice(f32[2,256,20,64]{1,0,3,2:T(2,128)} %get-tuple-element.384, f32[1,256,20,64]{1,0,3,2:T(1,128)S(1)} %copy.106, s32[]{:T(128)} %get-tuple-element.382, s32[]{:T(128)} %constant.66.clone.1..sunk, s32[]{:T(128)} %constant.66.clone.1..sunk, s32[]{:T(128)} %constant.66.clone.1..sunk) | dynamic-update-slice | bytes 2621444 | tf_op jit(solution)/shard_map/while/body/jit(dynamic_update_index_in_dim)/dynamic_update_slice | solution.py:118
  260.8 1.5 fusion.101
  264.7 27.0 %dynamic_update_slice.6 = f32[2,256,20,64]{1,0,3,2:T(2,128)} dynamic-update-slice(f32[2,256,20,64]{1,0,3,2:T(2,128)} %get-tuple-element.384, f32[1,256,20,64]{1,0,3,2:T(1,128)S(1)} %copy.106, s32[]{:T(128)} %get-tuple-element.382, s32[]{:T(128)} %constant.66.clone.1..sunk, s32[]{:T(128)} %constant.66.clone.1..sunk, s32[]{:T(128)} %constant.66.clone.1..sunk) | dynamic-update-slice | bytes 2621444 | tf_op jit(solution)/shard_map/while/body/jit(dynamic_update_index_in_dim)/dynamic_update_slice | solution.py:118
  297.2 21.1 %all-gather.1 = f32[8,1,20]{2,1,0:T(1,128)S(1)} all-gather(f32[1,1,20]{2,1,0:T(1,128)S(1)} %bitcast.198), channel_id=1, replica_groups=mesh['seq'=8,'grp'=4] {'seq'}, dimensions={0}, use_global_device_ids=true | all-gather | bytes 720 | tf_op jit(solution)/shard_map/all_gather | solution.py:20
  318.3 4.9 %reshape.128 = f32[512,20,64]{0,2,1:T(8,128)} reshape(f32[2,256,20,64]{1,0,3,2:T(2,128)} %get-tuple-element.147) | data formatting | bytes 5242880 | tf_op jit(solution)/shard_map/reshape | solution.py:137
  323.2 59.1 %all-gather.10.cloned.1.call-done = f32[160,64,128]{2,1,0:T(8,128)} async-done(((f32[20,64,128]{2,1,0:T(8,128)}), f32[160,64,128]{2,1,0:T(8,128)}) %all-gather.10.cloned.1.call-update) | async-done | bytes 5242896 | tf_op jit(solution)/shard_map/all_gather | solution.py:20
  382.3 10.2 %while.28 = (s32[]{:T(128)}, f32[20,64,128]{2,1,0:T(8,128)S(1)}, s32[]{:T(128)}, f32[8,20]{1,0:T(8,128)S(1)}, f32[8,20,64,128]{3,2,1,0:T(8,128)}, /*index=5*/s32[]{:T(128)}, s32[]{:T(128)}) while((s32[]{:T(128)}, f32[20,64,128]{2,1,0:T(8,128)S(1)}, s32[]{:T(128)}, f32[8,20]{1,0:T(8,128)S(1)}, f32[8,20,64,128]{3,2,1,0:T(8,128)}, ...), condition=%wide.region_8.9_spmd.clone, body=%wide.region_7.8_spmd.clone.sunk | while | flops 655364 | bytes 1966425 | solution.py:32
  392.5 3.9 multiply_reduce_fusion
  396.4 2.0 fusion.51
  398.4 5.7 %psum.7 = f32[512]{0:T(512)S(1)} all-reduce(f32[512]{0:T(512)S(1)} %get-tuple-element.278), channel_id=1, replica_groups=mesh['seq'=8,'grp'=4] {'grp'}, use_global_device_ids=true, to_apply=%region_10.11 | all-reduce | flops 512 | bytes 4096 | tf_op jit(solution)/shard_map/psum | solution.py:141
  404.1 33.1 %all-gather.8.cloned.1.call-done = bf16[512,5120]{0,1:T(8,128)(2,1)} async-done(((bf16[512,1280]{0,1:T(8,128)(2,1)}), bf16[512,5120]{0,1:T(8,128)(2,1)}) %all-gather.8.cloned.1.call-update) | async-done | bytes 5242896 | tf_op jit(solution)/shard_map/all_gather | solution.py:145
  437.2 9.6 %fusion.52 = bf16[512,640]{1,0:T(8,128)(2,1)} fusion(bf16[512,5120]{0,1:T(8,128)(2,1)} %all-gather.8.cloned.1.call-done, bf16[5120,640]{1,0:T(8,128)(2,1)} %param.27, f32[512]{0:T(512)S(1)} %add_rsqrt_fusion), kind=kOutput, calls=%fused_computation.80 | convolution fusion | flops 3356098560 | bytes 12453888 | tf_op jit(solution)/shard_map/dot_general | solution.py:144
  (138 shorter events, 34.1 us)
Async XLA Ops:
  6.5 9.9 %copy-start = (bf16[2560,20]{0,1:T(8,128)(2,1)S(1)}, bf16[2560,20]{0,1:T(8,128)(2,1)}, u32[]{:S(2)}) copy-start(bf16[2560,20]{0,1:T(8,128)(2,1)} %param.20) | copy-start | bytes 307204
  6.5 3.2 copy-start.6
  6.5 3.2 copy-start.16
  6.5 188.2 %all-gather.6.cloned.1.call-start = ((), (), s32[]{:S(2)}) async-start(), calls=%async_computation | async-start | bytes 14745600 | tf_op jit(solution)/shard_map/all_gather | solution.py:87
  7.3 375.0 %all-gather.10.cloned.1.call-start = ((), (), s32[]{:S(2)}) async-start(), calls=%async_computation.2 | async-start | bytes 5898240 | tf_op jit(solution)/shard_map/all_gather | solution.py:20
  7.3 2.5 copy-start.15
  9.8 5.9 %copy-start.14 = (bf16[4,2,128]{2,1,0:T(2,128)(2,1)S(1)}, bf16[4,2,128]{2,1,0:T(2,128)(2,1)}, u32[]{:S(2)}) copy-start(bf16[4,2,128]{2,1,0:T(2,128)(2,1)} %param.25) | copy-start | bytes 6148
  9.8 6.6 %copy-start.17 = (f32[20]{0:T(128)S(1)}, f32[20]{0:T(128)}, u32[]{:S(2)}) copy-start(f32[20]{0:T(128)} %param.21) | copy-start | bytes 244
  10.8 7.3 %collective-permute-start.1 = (bf16[3,2,128]{2,0,1:T(4,128)(2,1)S(1)}, bf16[3,2,128]{2,0,1:T(4,128)(2,1)S(1)}, u32[]{:S(2)}, u32[]{:S(2)}) collective-permute-start(bf16[3,2,128]{2,0,1:T(4,128)(2,1)S(1)} %slice_bitcast_fusion.2), channel_id=1, source_target_pairs={{0,4},{4,8},{8,12},{12,16},{16,20},{20,24},{24,28},{1,5},{5,9},{9,... | collective-permute-start | bytes 4616 | tf_op jit(solution)/shard_map/ppermute | solution.py:15
  15.7 2.3 copy-start.10
  19.5 0.7 copy-start.7
  209.0 4.8 %copy-start.3 = (bf16[512,2560]{0,1:T(8,128)(2,1)}, bf16[512,2560]{0,1:T(8,128)(2,1)S(1)}, u32[]{:S(2)}) copy-start(bf16[512,2560]{0,1:T(8,128)(2,1)S(1)} %copy.65) | copy-start | bytes 7864324
  209.1 8.7 %collective-permute-start = (bf16[3,1280]{0,1:T(8,128)(2,1)S(1)}, bf16[3,1280]{0,1:T(8,128)(2,1)S(1)}, u32[]{:S(2)}, u32[]{:S(2)}) collective-permute-start(bf16[3,1280]{0,1:T(8,128)(2,1)S(1)} %slice_bitcast_fusion.1), channel_id=1, source_target_pairs={{0,4},{4,8},{8,12},{12,16},{16,20},{20,24},{24,28},{1,5},{5,9},{9,... | collective-permute-start | bytes 23048 | tf_op jit(solution)/shard_map/ppermute | solution.py:15
  221.8 0.7 copy-start.11
  221.8 0.7 copy-start.12
  229.1 28.9 %copy-start.9 = (f32[2,256,20]{1,0,2:T(2,128)S(1)}, f32[2,256,20]{1,0,2:T(2,128)}, u32[]{:S(2)}) copy-start(f32[2,256,20]{1,0,2:T(2,128)} %copy-done.8) | copy-start | bytes 122884 | tf_op jit(solution)/shard_map/while
  258.0 0.6 copy-start.8
  264.7 28.9 %copy-start.9 = (f32[2,256,20]{1,0,2:T(2,128)S(1)}, f32[2,256,20]{1,0,2:T(2,128)}, u32[]{:S(2)}) copy-start(f32[2,256,20]{1,0,2:T(2,128)} %copy-done.8) | copy-start | bytes 122884 | tf_op jit(solution)/shard_map/while
  293.6 0.8 copy-start.2
  294.5 142.7 %all-gather.8.cloned.1.call-start = ((), (), s32[]{:S(2)}) async-start(), calls=%async_computation.1 | async-start | bytes 6553600 | tf_op jit(solution)/shard_map/all_gather | solution.py:145
  318.3 74.2 %copy-start.5 = (f32[512,1,1280]{0,2,1:T(8,128)S(1)}, f32[512,1,1280]{0,2,1:T(8,128)}, u32[]{:S(2)}) copy-start(f32[512,1,1280]{0,2,1:T(8,128)} %get-tuple-element.268) | copy-start | bytes 7864324
  392.4 4.0 copy-start.4
  392.4 4.0 copy-start.13
  437.2 9.6 %copy-start.1 = (bf16[2560,20]{0,1:T(8,128)(2,1)S(1)}, bf16[2560,20]{0,1:T(8,128)(2,1)}, u32[]{:S(2)}) copy-start(bf16[2560,20]{0,1:T(8,128)(2,1)} %param.20) | copy-start | bytes 307204
  (1 other events, 0.6 us)
Sparse Core Ops, SparseCore 0:
  9.5 185.2 all-gather.5
  294.6 87.5 all-gather.9
  398.5 38.5 all-gather.7
where the time goes:
time: 458 us; the launch traced here: 453 us
  waiting for transfers between devices  271 us (59%)
  local copies, waits for them, and re-layouts  71 us (16%)
  matrix products  35.7 us (8%)
  other arithmetic  27.3 us (6%)
  blocking collectives  26.8 us (6%)
  between operations  13.5 us (3%)
  starting transfers between devices  7.63 us (2%)
    all_gather x1, waiting for transfers between devices, body(): piece = lax.all_gather(inner_weight, 'seq', axis=2, tiled=True)  174 us
    all_gather x1, waiting for transfers between devices, prefix(): everything = jax.tree.map(lambda part: lax.all_gather(part, axis), value)  59.1 us
    dynamic_update_slice x4, local copies, waits for them, and re-layouts, body(): lax.scan(partial(span_step, decay_rate, skip_scale), initial, (xs_blocks,...  56.8 us
    all_gather x1, waiting for transfers between devices, body(): lax.all_gather(scaled, 'grp', axis=1, tiled=True)  33.1 us
    all_gather x1, blocking collectives, prefix(): everything = jax.tree.map(lambda part: lax.all_gather(part, axis), value)  21.1 us
    dot_general x1, matrix products, body(): jnp.dot(normed, flat, preferred_element_type=jnp.float32)  11.2 us
    select_n x8, other arithmetic, step(): return jax.tree.map(lambda a, b: jnp.where(reached, a, b), new, before)  9.86 us
    dot_general x1, matrix products, body(): jnp.dot(lax.all_gather(scaled, 'grp', axis=1, tiled=True), out_weight, pr...  9.57 us
  transfers between devices with their start and end apart: 5, of which 4 were waited for; matrix products, arithmetic and copies ran while one was open for 4% of the time, Pallas kernels for 0%

commit v1 on v0

--- a/solution.py
+++ b/solution.py
@@ -7,6 +7,24 @@
 SPAN = 256
 EPS = 1e-05
 HIGH = lax.Precision.HIGHEST
+
+
+def gather_around(array, axis, dim):
+    ways, here, step = (lax.axis_size(axis), lax.axis_index(axis), array.shape[dim])
+    shape = [n * ways if d == dim else n for d, n in enumerate(array.shape)]
+    full = lax.dynamic_update_slice_in_dim(
+        jnp.zeros(shape, array.dtype), array, here * step, axis=dim
+    )
+    going_up = going_down = array
+    for far in range(1, ways // 2 + 1):
+        going_up = lax.ppermute(going_up, axis, [(d, (d + 1) % ways) for d in range(ways)])
+        full = lax.dynamic_update_slice_in_dim(full, going_up, (here - far) % ways * step, axis=dim)
+        if 2 * far < ways:
+            going_down = lax.ppermute(going_down, axis, [(d, (d - 1) % ways) for d in range(ways)])
+            full = lax.dynamic_update_slice_in_dim(
+                full, going_down, (here + far) % ways * step, axis=dim
+            )
+    return full
 
 
 def from_behind(value, axis, steps):
@@ -84,7 +102,7 @@
     normed = (
         wide * lax.rsqrt(jnp.mean(wide * wide, axis=1, keepdims=True) + EPS) * norm_gain
     ).astype(jnp.bfloat16)
-    piece = lax.all_gather(inner_weight, "seq", axis=2, tiled=True)
+    piece = gather_around(inner_weight, "seq", 2)
     count = piece.shape[2]
     flat = piece.reshape(piece.shape[0], 2 * count)
     result = jnp.dot(normed, flat, preferred_element_type=jnp.float32).astype(jnp.bfloat16)

time: 458 us -> 524 us (1.14)
  waiting for transfers between devices: 271 us -> 296 us
  local copies, waits for them, and re-layouts: 71 us -> 93.6 us
  starting transfers between devices: 7.63 us -> 23.1 us
    ppermute x0 -> x7, waiting for transfers between devices: none -> 203 us  [the longest x4 202 us: gather_around(): lax.ppermute(going_up, axis, [(d, (d + 1) % ways) for d in range(ways)])]
    all_gather x1 -> x0, waiting for transfers between devices: 174 us -> none  [body(): piece = lax.all_gather(inner_weight, 'seq', axis=2, tiled=True)]
    ppermute x0 -> x7, starting transfers between devices: none -> 19 us  [the longest x4 10.4 us: gather_around(): lax.ppermute(going_up, axis, [(d, (d + 1) % ways) for d in range(ways)])]
    dynamic_update_slice x0 -> x8, local copies, waits for them, and re-layouts: none -> 17.6 us  [the longest x4 8.02 us: gather_around(): lax.dynamic_update_slice_in_dim(full, going_up, (here - far) % ways * ste...]
    broadcast_in_dim x0 -> x1, local copies, waits for them, and re-layouts: none -> 5.51 us  [gather_around(): jnp.zeros(shape, array.dtype)]
  transfers between devices with their start and end apart: 5 -> 11, of which waited for: 4 -> 7; matrix products, arithmetic and copies ran while one was open for 4% -> 8% of each run, Pallas kernels for 0% -> 0%
where the time goes in v1:
time: 524 us; the launch traced here: 519 us
  waiting for transfers between devices  296 us (56%)
  local copies, waits for them, and re-layouts  93.6 us (18%)
  matrix products  37.1 us (7%)
  blocking collectives  27.5 us (5%)
  other arithmetic  27.3 us (5%)
  starting transfers between devices  23.1 us (4%)
  between operations  13.9 us (3%)
    ppermute x4, waiting for transfers between devices, gather_around(): lax.ppermute(going_up, axis, [(d, (d + 1) % ways) for d in range(ways)])  202 us
    all_gather x1, waiting for transfers between devices, prefix(): everything = jax.tree.map(lambda part: lax.all_gather(part, axis), value)  58.2 us
    dynamic_update_slice x4, local copies, waits for them, and re-layouts, body(): lax.scan(partial(span_step, decay_rate, skip_scale), initial, (xs_blocks,...  56.8 us
    all_gather x1, waiting for transfers between devices, body(): lax.all_gather(scaled, 'grp', axis=1, tiled=True)  33.1 us
    all_gather x1, blocking collectives, prefix(): everything = jax.tree.map(lambda part: lax.all_gather(part, axis), value)  21.9 us
    dot_general x1, matrix products, body(): jnp.dot(normed, flat, preferred_element_type=jnp.float32)  11.2 us
  transfers between devices with their start and end apart: 11, of which 7 were waited for; matrix products, arithmetic and copies ran while one was open for 8% of the time, Pallas kernels for 0%

profile of v1, /device:TPU:0, one launch (start us, length us, event | category | flops | bytes accessed | tf_op | source)
XLA Modules:
  0.0 519.1 jit_solution(16606516852513915350)
XLA Ops:
  6.5 3.0 collective-permute-start
  9.5 3.1 collective-permute-start.1
  12.6 67.4 %collective-permute-done = bf16[2560,2,160]{0,2,1:T(8,128)(2,1)S(1)} collective-permute-done((bf16[2560,2,160]{0,2,1:T(8,128)(2,1)}, bf16[2560,2,160]{0,2,1:T(8,128)(2,1)S(1)}, u32[]{:S(2)}, u32[]{:S(2)}) %collective-permute-start) | collective-permute-done | bytes 1638432 | tf_op jit(solution)/shard_map/ppermute | solution.py:20
  93.6 58.1 %collective-permute-done.2 = bf16[2560,2,160]{0,2,1:T(8,128)(2,1)} collective-permute-done((bf16[2560,2,160]{0,2,1:T(8,128)(2,1)S(1)}, bf16[2560,2,160]{0,2,1:T(8,128)(2,1)}, u32[]{:S(2)}, u32[]{:S(2)}) %collective-permute-start.2) | collective-permute-done | bytes 1638432 | tf_op jit(solution)/shard_map/ppermute | solution.py:20
  155.2 5.5 %broadcast_in_dim.18 = bf16[2560,2,1280]{0,2,1:T(8,128)(2,1)} broadcast(bf16[]{:T(256)} %constant.115.clone.1), dimensions={} | broadcast | bytes 13107202 | tf_op jit(solution)/shard_map/broadcast_in_dim | solution.py:16
  160.7 2.8 constant_dynamic-update-slice_fusion.7
  165.8 3.1 collective-permute-start.5
  170.3 52.8 %collective-permute-done.4 = bf16[2560,2,160]{0,2,1:T(8,128)(2,1)} collective-permute-done((bf16[2560,2,160]{0,2,1:T(8,128)(2,1)}, bf16[2560,2,160]{0,2,1:T(8,128)(2,1)}, u32[]{:S(2)}, u32[]{:S(2)}) %collective-permute-start.4) | collective-permute-done | bytes 1638432 | tf_op jit(solution)/shard_map/ppermute | solution.py:20
  231.0 2.8 constant_dynamic-update-slice_fusion.3
  237.8 24.2 %collective-permute-done.6 = bf16[2560,2,160]{0,2,1:T(8,128)(2,1)S(1)} collective-permute-done((bf16[2560,2,160]{0,2,1:T(8,128)(2,1)}, bf16[2560,2,160]{0,2,1:T(8,128)(2,1)S(1)}, u32[]{:S(2)}, u32[]{:S(2)}) %collective-permute-start.6) | collective-permute-done | bytes 1638432 | tf_op jit(solution)/shard_map/ppermute | solution.py:20
  263.3 11.2 %convolution_convert_fusion = bf16[512,2560]{1,0:T(8,128)(2,1)} fusion(bf16[2560,2560]{0,1:T(8,128)(2,1)} %bitcast.185, bf16[512,2560]{1,0:T(8,128)(2,1)S(1)} %copy-done.6, f32[2560]{0:T(1024)S(1)} %copy-done.17, f32[512]{0:T(512)S(1)} %add_rsqrt_fusion.1), kind=kOutput, calls=%fused_computation.59 | convolution fusion | flops 6717440000 | bytes 18362368 | tf_op jit(solution)/shard_map/dot_general | solution.py:108
  274.5 3.0 copy.65
  284.2 3.2 multiply_convert_fusion.8
  288.1 71.2 %while.27 = (s32[]{:T(128)}, f32[20,64,128]{2,1,0:T(8,128)S(1)}, f32[2,256,20,64]{1,0,3,2:T(2,128)}, f32[2,256,20]{1,0,2:T(2,128)S(1)}, f32[20]{0:T(128)S(1)}, /...) while((s32[]{:T(128)}, f32[20,64,128]{2,1,0:T(8,128)S(1)}, ...), condition=%wide.region_4.5_spmd.clone, body=%wide.region_1.4_spmd.clone.sunk | while | flops 782684224 | bytes 15246184 | solution.py:136
  294.8 27.0 %dynamic_update_slice.46 = f32[2,256,20,64]{1,0,3,2:T(2,128)} dynamic-update-slice(f32[2,256,20,64]{1,0,3,2:T(2,128)} %get-tuple-element.384, f32[1,256,20,64]{1,0,3,2:T(1,128)S(1)} %copy.106, s32[]{:T(128)} %get-tuple-element.382, s32[]{:T(128)} %constant.111.clone.1..sunk, s32[]{:T(128)} %constant.111.clone.1..sunk, s32[]{:T(128)} %constant.111.clone.1..sunk) | dynamic-update-slice | bytes 2621444 | tf_op jit(solution)/shard_map/while/body/jit(dynamic_update_index_in_dim)/dynamic_update_slice | solution.py:136
  330.4 27.0 %dynamic_update_slice.46 = f32[2,256,20,64]{1,0,3,2:T(2,128)} dynamic-update-slice(f32[2,256,20,64]{1,0,3,2:T(2,128)} %get-tuple-element.384, f32[1,256,20,64]{1,0,3,2:T(1,128)S(1)} %copy.106, s32[]{:T(128)} %get-tuple-element.382, s32[]{:T(128)} %constant.111.clone.1..sunk, s32[]{:T(128)} %constant.111.clone.1..sunk, s32[]{:T(128)} %constant.111.clone.1..sunk) | dynamic-update-slice | bytes 2621444 | tf_op jit(solution)/shard_map/while/body/jit(dynamic_update_index_in_dim)/dynamic_update_slice | solution.py:136
  362.8 21.9 %all-gather.1 = f32[8,1,20]{2,1,0:T(1,128)S(1)} all-gather(f32[1,1,20]{2,1,0:T(1,128)S(1)} %bitcast.199), channel_id=1, replica_groups=mesh['seq'=8,'grp'=4] {'seq'}, dimensions={0}, use_global_device_ids=true | all-gather | bytes 720 | tf_op jit(solution)/shard_map/all_gather | solution.py:38
  384.7 4.9 reshape.128
  389.6 58.2 %all-gather.7.cloned.1.call-done = f32[160,64,128]{2,1,0:T(8,128)} async-done(((f32[20,64,128]{2,1,0:T(8,128)}), f32[160,64,128]{2,1,0:T(8,128)}) %all-gather.7.cloned.1.call-update) | async-done | bytes 5242896 | tf_op jit(solution)/shard_map/all_gather | solution.py:38
  447.8 10.2 %while.28 = (s32[]{:T(128)}, f32[20,64,128]{2,1,0:T(8,128)S(1)}, s32[]{:T(128)}, f32[8,20]{1,0:T(8,128)S(1)}, f32[8,20,64,128]{3,2,1,0:T(8,128)}, /*index=5*/s32[]{:T(128)}, s32[]{:T(128)}) while((s32[]{:T(128)}, f32[20,64,128]{2,1,0:T(8,128)S(1)}, s32[]{:T(128)}, f32[8,20]{1,0:T(8,128)S(1)}, f32[8,20,64,128]{3,2,1,0:T(8,128)}, ...), condition=%wide.region_8.9_spmd.clone, body=%wide.region_7.8_spmd.clone.sunk | while | flops 655364 | bytes 1966425 | solution.py:50
  458.0 3.9 multiply_reduce_fusion
  464.0 5.7 %psum.7 = f32[512]{0:T(512)S(1)} all-reduce(f32[512]{0:T(512)S(1)} %get-tuple-element.278), channel_id=1, replica_groups=mesh['seq'=8,'grp'=4] {'grp'}, use_global_device_ids=true, to_apply=%region_10.11 | all-reduce | flops 512 | bytes 4096 | tf_op jit(solution)/shard_map/psum | solution.py:159
  469.7 33.1 %all-gather.5.cloned.1.call-done = bf16[512,5120]{0,1:T(8,128)(2,1)} async-done(((bf16[512,1280]{0,1:T(8,128)(2,1)}), bf16[512,5120]{0,1:T(8,128)(2,1)}) %all-gather.5.cloned.1.call-update) | async-done | bytes 5242896 | tf_op jit(solution)/shard_map/all_gather | solution.py:163
  502.7 9.6 %fusion.52 = bf16[512,640]{1,0:T(8,128)(2,1)} fusion(bf16[512,5120]{0,1:T(8,128)(2,1)} %all-gather.5.cloned.1.call-done, bf16[5120,640]{1,0:T(8,128)(2,1)} %param.27, f32[512]{0:T(512)S(1)} %add_rsqrt_fusion), kind=kOutput, calls=%fused_computation.80 | convolution fusion | flops 3356098560 | bytes 12453888 | tf_op jit(solution)/shard_map/dot_general | solution.py:162
  (160 shorter events, 73.4 us)
Async XLA Ops:
  6.5 85.6 %copy-start = (bf16[2560,20]{0,1:T(8,128)(2,1)S(1)}, bf16[2560,20]{0,1:T(8,128)(2,1)}, u32[]{:S(2)}) copy-start(bf16[2560,20]{0,1:T(8,128)(2,1)} %param.20) | copy-start | bytes 307204
  6.5 78.2 %copy-start.6 = (bf16[512,2560]{1,0:T(8,128)(2,1)S(1)}, bf16[512,2560]{1,0:T(8,128)(2,1)}, u32[]{:S(2)}) copy-start(bf16[512,2560]{1,0:T(8,128)(2,1)} %param.16) | copy-start | bytes 7864324
  6.5 441.3 %all-gather.7.cloned.1.call-start = ((), (), s32[]{:S(2)}) async-start(), calls=%async_computation.1 | async-start | bytes 5898240 | tf_op jit(solution)/shard_map/all_gather | solution.py:38
  6.5 73.5 %collective-permute-start = (bf16[2560,2,160]{0,2,1:T(8,128)(2,1)}, bf16[2560,2,160]{0,2,1:T(8,128)(2,1)S(1)}, u32[]{:S(2)}, u32[]{:S(2)}) collective-permute-start(bf16[2560,2,160]{0,2,1:T(8,128)(2,1)} %param.18), channel_id=1, source_target_pairs={{0,4},{4,8},{8,12},{12,16},{16,20},{20,24},{24,28},{28,0},{1,5},{5... | collective-permute-start | bytes 4915208 | tf_op jit(solution)/shard_map/ppermute | solution.py:20
  9.5 80.2 %collective-permute-start.1 = (bf16[2560,2,160]{0,2,1:T(8,128)(2,1)}, bf16[2560,2,160]{0,2,1:T(8,128)(2,1)}, u32[]{:S(2)}, u32[]{:S(2)}) collective-permute-start(bf16[2560,2,160]{0,2,1:T(8,128)(2,1)} %param.18), channel_id=1, source_target_pairs={{0,28},{4,0},{8,4},{12,8},{16,12},{20,16},{24,20},{28,24},{1,29},{... | collective-permute-start | bytes 4915208 | tf_op jit(solution)/shard_map/ppermute | solution.py:23
  80.0 7.0 %copy-start.7 = (bf16[2560,2,160]{0,2,1:T(8,128)(2,1)}, bf16[2560,2,160]{0,2,1:T(8,128)(2,1)S(1)}, u32[]{:S(2)}) copy-start(bf16[2560,2,160]{0,2,1:T(8,128)(2,1)S(1)} %collective-permute-done) | copy-start | bytes 4915204
  80.0 71.7 %collective-permute-start.2 = (bf16[2560,2,160]{0,2,1:T(8,128)(2,1)S(1)}, bf16[2560,2,160]{0,2,1:T(8,128)(2,1)}, u32[]{:S(2)}, u32[]{:S(2)}) collective-permute-start(bf16[2560,2,160]{0,2,1:T(8,128)(2,1)S(1)} %collective-permute-done), channel_id=1, source_target_pairs={{0,4},{4,8},{8,12},{12,16},{16,20},{20,24},{24,28},{28,0},{1,5},{5... | collective-permute-start | bytes 4915208 | tf_op jit(solution)/shard_map/ppermute | solution.py:20
  84.7 4.9 copy-start.16
  84.8 7.4 %copy-start.17 = (f32[2560]{0:T(1024)S(1)}, f32[2560]{0:T(1024)}, u32[]{:S(2)}) copy-start(f32[2560]{0:T(1024)} %param.17) | copy-start | bytes 30724
  84.8 7.4 %copy-start.18 = (f32[20]{0:T(128)S(1)}, f32[20]{0:T(128)}, u32[]{:S(2)}) copy-start(f32[20]{0:T(128)} %param.21) | copy-start | bytes 244
  87.1 67.3 %copy-start.12 = (bf16[4,1280]{1,0:T(4,128)(2,1)S(1)}, bf16[4,1280]{1,0:T(4,128)(2,1)}, u32[]{:S(2)}) copy-start(bf16[4,1280]{1,0:T(4,128)(2,1)} %param.24) | copy-start | bytes 30724
  87.1 76.5 %collective-permute-start.8 = (bf16[3,2,128]{2,0,1:T(4,128)(2,1)S(1)}, bf16[3,2,128]{2,0,1:T(4,128)(2,1)S(1)}, u32[]{:S(2)}, u32[]{:S(2)}) collective-permute-start(bf16[3,2,128]{2,0,1:T(4,128)(2,1)S(1)} %slice_bitcast_fusion.2), channel_id=1, source_target_pairs={{0,4},{4,8},{8,12},{12,16},{16,20},{20,24},{24,28},{1,5},{5,9},{9,... | collective-permute-start | bytes 4616 | tf_op jit(solution)/shard_map/ppermute | solution.py:33
  89.7 76.1 %collective-permute-start.3 = (bf16[2560,2,160]{0,2,1:T(8,128)(2,1)}, bf16[2560,2,160]{0,2,1:T(8,128)(2,1)}, u32[]{:S(2)}, u32[]{:S(2)}) collective-permute-start(bf16[2560,2,160]{0,2,1:T(8,128)(2,1)} %collective-permute-done.1), channel_id=1, source_target_pairs={{0,28},{4,0},{8,4},{12,8},{16,12},{20,16},{24,20},{28,24},{1,29},{... | collective-permute-start | bytes 4915208 | tf_op jit(solution)/shard_map/ppermute | solution.py:23
  151.7 71.3 %collective-permute-start.4 = (bf16[2560,2,160]{0,2,1:T(8,128)(2,1)}, bf16[2560,2,160]{0,2,1:T(8,128)(2,1)}, u32[]{:S(2)}, u32[]{:S(2)}) collective-permute-start(bf16[2560,2,160]{0,2,1:T(8,128)(2,1)} %collective-permute-done.2), channel_id=1, source_target_pairs={{0,4},{4,8},{8,12},{12,16},{16,20},{20,24},{24,28},{28,0},{1,5},{5... | collective-permute-start | bytes 4915208 | tf_op jit(solution)/shard_map/ppermute | solution.py:20
  163.5 5.4 %copy-start.8 = (bf16[2560,2,160]{0,2,1:T(8,128)(2,1)S(1)}, bf16[2560,2,160]{0,2,1:T(8,128)(2,1)}, u32[]{:S(2)}) copy-start(bf16[2560,2,160]{0,2,1:T(8,128)(2,1)} %copy-done.7) | copy-start | bytes 4915204
  165.8 70.6 %collective-permute-start.5 = (bf16[2560,2,160]{0,2,1:T(8,128)(2,1)}, bf16[2560,2,160]{0,2,1:T(8,128)(2,1)S(1)}, u32[]{:S(2)}, u32[]{:S(2)}) collective-permute-start(bf16[2560,2,160]{0,2,1:T(8,128)(2,1)} %collective-permute-done.3), channel_id=1, source_target_pairs={{0,28},{4,0},{8,4},{12,8},{16,12},{20,16},{24,20},{28,24},{1,29},{... | collective-permute-start | bytes 4915208 | tf_op jit(solution)/shard_map/ppermute | solution.py:23
  223.1 38.9 %collective-permute-start.6 = (bf16[2560,2,160]{0,2,1:T(8,128)(2,1)}, bf16[2560,2,160]{0,2,1:T(8,128)(2,1)S(1)}, u32[]{:S(2)}, u32[]{:S(2)}) collective-permute-start(bf16[2560,2,160]{0,2,1:T(8,128)(2,1)} %collective-permute-done.4), channel_id=1, source_target_pairs={{0,4},{4,8},{8,12},{12,16},{16,20},{20,24},{24,28},{28,0},{1,5},{5... | collective-permute-start | bytes 4915208 | tf_op jit(solution)/shard_map/ppermute | solution.py:20
  277.6 5.9 %collective-permute-start.7 = (bf16[3,1280]{0,1:T(8,128)(2,1)S(1)}, bf16[3,1280]{0,1:T(8,128)(2,1)S(1)}, u32[]{:S(2)}, u32[]{:S(2)}) collective-permute-start(bf16[3,1280]{0,1:T(8,128)(2,1)S(1)} %slice_bitcast_fusion.1), channel_id=1, source_target_pairs={{0,4},{4,8},{8,12},{12,16},{16,20},{20,24},{24,28},{1,5},{5,9},{9,... | collective-permute-start | bytes 23048 | tf_op jit(solution)/shard_map/ppermute | solution.py:33
  294.8 28.9 %copy-start.11 = (f32[2,256,20]{1,0,2:T(2,128)S(1)}, f32[2,256,20]{1,0,2:T(2,128)}, u32[]{:S(2)}) copy-start(f32[2,256,20]{1,0,2:T(2,128)} %copy-done.10) | copy-start | bytes 122884 | tf_op jit(solution)/shard_map/while
  330.4 28.9 %copy-start.11 = (f32[2,256,20]{1,0,2:T(2,128)S(1)}, f32[2,256,20]{1,0,2:T(2,128)}, u32[]{:S(2)}) copy-start(f32[2,256,20]{1,0,2:T(2,128)} %copy-done.10) | copy-start | bytes 122884 | tf_op jit(solution)/shard_map/while
  360.2 142.6 %all-gather.5.cloned.1.call-start = ((), (), s32[]{:S(2)}) async-start(), calls=%async_computation | async-start | bytes 6553600 | tf_op jit(solution)/shard_map/all_gather | solution.py:163
  384.7 73.3 %copy-start.5 = (f32[512,1,1280]{0,2,1:T(8,128)S(1)}, f32[512,1,1280]{0,2,1:T(8,128)}, u32[]{:S(2)}) copy-start(f32[512,1,1280]{0,2,1:T(8,128)} %get-tuple-element.268) | copy-start | bytes 7864324
  458.0 4.0 copy-start.4
  502.7 9.6 %copy-start.1 = (bf16[2560,20]{0,1:T(8,128)(2,1)S(1)}, bf16[2560,20]{0,1:T(8,128)(2,1)}, u32[]{:S(2)}) copy-start(bf16[2560,20]{0,1:T(8,128)(2,1)} %param.20) | copy-start | bytes 307204
  (8 other events, 11.8 us)
Sparse Core Ops, SparseCore 0:
  360.3 87.4 all-gather.6
  464.1 38.5 all-gather.4
